TPU v7x, 32 devices: a whole 2x2x4 slice. The times are simulated.
32 devices in a mesh: rep: 4 (over x, core), fsdp: 8 (over z, y).
Axes of the slice: x: 2, y: 2, z: 4, core: 2. Of those that a mesh axis runs over, the one named last changes fastest.
Arguments:
- tokens: bfloat16 [32768, 1024], P(('rep', 'fsdp')), may hold values from -6 to 6
- cotangent: bfloat16 [32768, 1024], P(('rep', 'fsdp')), may hold values from -6 to 6
- segment_ids: int32 [32, 1024], P(('rep', 'fsdp')), may hold values from 0 to 15, never falling along the last dimension, each value on 1 to 512 neighbouring positions
- attention_weight: float32 [4, 1024, 1024], P(None, 'fsdp'), may hold values from -0.375 to 0.375
- attention_momentum: float32 [4, 1024, 1024], P(None, 'fsdp'), may hold values from -0.1875 to 0.1875
- attention_first: float32 [4, 4, 1024, 1024], P('rep', None, 'fsdp'), may hold values from -112 to 112
- attention_second: float32 [4, 4, 1024, 1024], P('rep', None, 'fsdp'), may hold values from 54.8864 to 876.544
- expand_weight: float32 [1024, 4096], P('fsdp'), may hold values from -0.1875 to 0.1875
- expand_momentum: float32 [1024, 4096], P('fsdp'), may hold values from -0.1875 to 0.1875
- expand_first: float32 [4, 1024, 4096], P('rep', 'fsdp'), may hold values from -128 to 128
- expand_second: float32 [4, 1024, 4096], P('rep', 'fsdp'), may hold values from 85.1968 to 1368.064
- contract_weight: float32 [4096, 1024], P('fsdp'), may hold values from -0.09375 to 0.09375
- contract_momentum: float32 [4096, 1024], P('fsdp'), may hold values from -0.09375 to 0.09375
- contract_first: float32 [4, 4096, 1024], P('rep', 'fsdp'), may hold values from -256 to 256
- contract_second: float32 [4, 4096, 1024], P('rep', 'fsdp'), may hold values from 341.6064 to 5464.064
- vectors: float32 [12, 1024], P(None, 'fsdp'), may hold values from -0.6 to 1.4
- vectors_momentum: float32 [12, 1024], P(None, 'fsdp'), may hold values from -1.25 to 1.25
- vectors_first: float32 [4, 12, 1024], P('rep', None, 'fsdp'), may hold values from -448 to 448
- vectors_second: float32 [4, 12, 1024], P('rep', None, 'fsdp'), may hold values from 876.544 to 14008.32
Outputs:
- layer_output: bfloat16 [32768, 1024], P(('rep', 'fsdp'))
- input_grad: bfloat16 [32768, 1024], P(('rep', 'fsdp'))
- attention_first_new: float32 [4, 4, 1024, 1024], P('rep', None, 'fsdp')
- attention_second_new: float32 [4, 4, 1024, 1024], P('rep', None, 'fsdp')
- outer_attention: float32 [3, 4, 1024, 1024], P(None, None, 'fsdp')
- copy_attention: bfloat16 [4, 1024, 1024], P(None, 'fsdp')
- expand_first_new: float32 [4, 1024, 4096], P('rep', 'fsdp')
- expand_second_new: float32 [4, 1024, 4096], P('rep', 'fsdp')
- outer_expand: float32 [3, 1024, 4096], P(None, 'fsdp')
- copy_expand: bfloat16 [1024, 4096], P('fsdp')
- contract_first_new: float32 [4, 4096, 1024], P('rep', 'fsdp')
- contract_second_new: float32 [4, 4096, 1024], P('rep', 'fsdp')
- outer_contract: float32 [3, 4096, 1024], P(None, 'fsdp')
- copy_contract: bfloat16 [4096, 1024], P('fsdp')
- vectors_first_new: float32 [4, 12, 1024], P('rep', None, 'fsdp')
- vectors_second_new: float32 [4, 12, 1024], P('rep', None, 'fsdp')
- outer_vectors: float32 [3, 12, 1024], P(None, None, 'fsdp')
- copy_vectors: bfloat16 [12, 1024], P(None, 'fsdp')
Inputs may be any that keep to these rules, and one draw needn't show every extreme that they name: `segment_ids`: within a row the numbers never fall; a run of equal numbers is one document, and tokens attend only within their document.
All inputs are finite; a program needn't handle non-finite values.
Results may differ from a plain program's by a relative error of at most 0.012.
The roundings to bfloat16 on the way count: a program that leaves them out, or rounds other values in their place, can miss the bound.
Values may be sent and summed in bfloat16 or wider, within the bound.
A program may use at most 448 MiB of HBM per device.

v0:
```python
from functools import partial
import jax
import jax.numpy as jnp
from jax import lax
from jax.sharding import PartitionSpec as P

D = 1024
H = 16
HD = 64
FF = 4096
LEN = 1024
SEQ_DEV = 1
ADAM_STEP = 4
TOK_DEV = 1024


def norm_forward(values_in, gain_row, shift_row):
    center = values_in - jnp.mean(values_in, axis=-1, keepdims=True)
    inv_scale = lax.rsqrt(jnp.mean(center * center, axis=-1, keepdims=True) + 1e-05)
    normed = center * inv_scale
    return (normed * gain_row + shift_row, normed, inv_scale)


def norm_backward(grad_out, normed, inv_scale, gain_row):
    grad_gain = jnp.sum(grad_out * normed, axis=0)
    grad_shift = jnp.sum(grad_out, axis=0)
    scaled_grad = grad_out * gain_row
    grad_value = inv_scale * (
        scaled_grad
        - jnp.mean(scaled_grad, axis=-1, keepdims=True)
        - normed * jnp.mean(scaled_grad * normed, axis=-1, keepdims=True)
    )
    return (grad_value, grad_gain, grad_shift)


def product_over(left, right):
    return lax.dot_general(
        left, right, (((0,), (0,)), ((), ())), preferred_element_type=jnp.float32
    )


def product_back(left, right):
    return lax.dot_general(
        left, right, (((1,), (1,)), ((), ())), preferred_element_type=jnp.float32
    )


def block_scores(query_block, key_block, row_segments, all_segments):
    scores = jnp.einsum("qhd,khd->hqk", query_block, key_block, preferred_element_type=jnp.float32)
    same_doc = row_segments[:, None] == all_segments[None, :]
    return jnp.where(same_doc[None], scores, -1e30)


def inner_step(weight, gradient, first_moment, second_moment, learn_rate, weight_decay):
    first_new = 0.5 * first_moment + 0.5 * gradient
    second_new = 0.75 * second_moment + 0.25 * gradient * gradient
    update_dir = (
        first_new
        / (1.0 - 0.5**ADAM_STEP)
        / (jnp.sqrt(second_new / (1.0 - 0.75**ADAM_STEP)) + 1e-08)
    )
    return (weight - learn_rate * (update_dir + weight_decay * weight), first_new, second_new)


def per_device(
    tokens,
    cotangent,
    segment_ids,
    attention_weight,
    attention_momentum,
    attention_first,
    attention_second,
    expand_weight,
    expand_momentum,
    expand_first,
    expand_second,
    contract_weight,
    contract_momentum,
    contract_first,
    contract_second,
    vectors,
    vectors_momentum,
    vectors_first,
    vectors_second,
):
    attn_full, vector_full = (
        lax.all_gather(attention_weight.astype(jnp.bfloat16), "fsdp", axis=1, tiled=True),
        lax.all_gather(vectors.astype(jnp.bfloat16), "fsdp", axis=1, tiled=True),
    )
    vector_rows = vector_full.astype(jnp.float32)
    gain_one, gain_two, shift_one, shift_two = (
        vector_rows[0],
        vector_rows[1],
        vector_rows[2],
        vector_rows[3],
    )
    bias_query, bias_value, bias_mixed, bias_down = (
        vector_rows[4],
        vector_rows[5],
        vector_rows[6],
        vector_rows[7],
    )
    bias_up = vector_rows[8:].reshape(FF)
    projected = jnp.einsum("td,nde->nte", tokens, attn_full[:3], preferred_element_type=jnp.float32)
    query_all = ((projected[0] + bias_query) * 0.125).astype(jnp.bfloat16)
    key_all = projected[1].astype(jnp.bfloat16)
    value_all = (projected[2] + bias_value).astype(jnp.bfloat16)
    query_heads = query_all.reshape(SEQ_DEV, LEN, H, HD)
    key_heads = key_all.reshape(SEQ_DEV, LEN, H, HD)
    value_heads = value_all.reshape(SEQ_DEV, LEN, H, HD)
    block_rows = min(512, LEN)
    head_group = min(8, H)
    context_rows = []
    log_sums = []
    seq_index = 0
    for row_start in range(0, LEN, block_rows):
        block_pieces = []
        for head_start in range(0, H, head_group):
            head_part = slice(head_start, head_start + head_group)
            scores = block_scores(
                query_heads[seq_index, row_start : row_start + block_rows, head_part],
                key_heads[seq_index, :, head_part],
                segment_ids[seq_index, row_start : row_start + block_rows],
                segment_ids[seq_index],
            )
            row_max = jnp.max(scores, axis=-1, keepdims=True)
            exp_score = jnp.exp(scores - row_max)
            row_total = jnp.sum(exp_score, axis=-1, keepdims=True)
            probability = (exp_score / row_total).astype(jnp.bfloat16)
            block_pieces.append(
                jnp.einsum(
                    "hqk,khd->qhd",
                    probability,
                    value_heads[seq_index, :, head_part],
                    preferred_element_type=jnp.float32,
                )
            )
            log_sums.append(row_max + jnp.log(row_total))
        context_rows.append(jnp.concatenate(block_pieces, axis=1))
    mixed = jnp.concatenate(context_rows, axis=0).reshape(TOK_DEV, D).astype(jnp.bfloat16)
    attn_out = jnp.dot(mixed, attn_full[3], preferred_element_type=jnp.float32) + bias_mixed
    hidden, normed_one, scale_one = norm_forward(
        tokens.astype(jnp.float32) + attn_out, gain_one, shift_one
    )
    hidden_low = hidden.astype(jnp.bfloat16)
    ffn_expand, ffn_contract = (
        lax.all_gather(expand_weight.astype(jnp.bfloat16), "fsdp", axis=0, tiled=True),
        lax.all_gather(contract_weight.astype(jnp.bfloat16), "fsdp", axis=0, tiled=True),
    )
    pre_act = jnp.dot(hidden_low, ffn_expand, preferred_element_type=jnp.float32) + bias_up
    activated = jax.nn.gelu(pre_act, approximate=False).astype(jnp.bfloat16)
    branch = jnp.dot(activated, ffn_contract, preferred_element_type=jnp.float32) + bias_down
    layer_output, normed_two, scale_two = norm_forward(hidden + branch, gain_two, shift_two)
    grad_sum, grad_gain_two, grad_shift_two = norm_backward(
        cotangent.astype(jnp.float32), normed_two, scale_two, gain_two
    )
    grad_branch = grad_sum.astype(jnp.bfloat16)
    grad_act = product_back(grad_branch, ffn_contract)
    unused_value, gelu_pull = jax.vjp(partial(jax.nn.gelu, approximate=False), pre_act)
    grad_pre_low = gelu_pull(grad_act)[0].astype(jnp.bfloat16)
    grad_hidden = grad_sum + product_back(grad_pre_low, ffn_expand)
    contract_full = product_over(activated, grad_branch)
    expand_full = product_over(hidden_low, grad_pre_low)
    grad_expand, grad_contract = (
        lax.psum_scatter(expand_full, "fsdp", scatter_dimension=0, tiled=True),
        lax.psum_scatter(contract_full, "fsdp", scatter_dimension=0, tiled=True),
    )
    grad_resid, grad_gain_one, grad_shift_one = norm_backward(
        grad_hidden, normed_one, scale_one, gain_one
    )
    grad_attn_out = grad_resid.astype(jnp.bfloat16)
    grad_bias_mixed = jnp.sum(grad_attn_out.astype(jnp.float32), axis=0)
    grad_output_proj = product_over(mixed, grad_attn_out)
    grad_mixed = product_back(grad_attn_out, attn_full[3]).astype(jnp.bfloat16)
    grad_context = grad_mixed.reshape(SEQ_DEV, LEN, H, HD)
    query_grads = []
    lse_index = 0
    seq_index = 0
    key_totals = [
        jnp.zeros((LEN, head_group, HD), jnp.float32) for head_start in range(0, H, head_group)
    ]
    value_totals = [
        jnp.zeros((LEN, head_group, HD), jnp.float32) for head_start in range(0, H, head_group)
    ]
    for row_start in range(0, LEN, block_rows):
        block_pieces = []
        for group_index, head_start in enumerate(range(0, H, head_group)):
            head_part = slice(head_start, head_start + head_group)
            query_block = query_heads[seq_index, row_start : row_start + block_rows, head_part]
            key_block = key_heads[seq_index, :, head_part]
            value_block = value_heads[seq_index, :, head_part]
            ctx_grad = grad_context[seq_index, row_start : row_start + block_rows, head_part]
            scores = block_scores(
                query_block,
                key_block,
                segment_ids[seq_index, row_start : row_start + block_rows],
                segment_ids[seq_index],
            )
            probability = jnp.exp(scores - log_sums[lse_index])
            lse_index = lse_index + 1
            value_totals[group_index] = value_totals[group_index] + jnp.einsum(
                "hqk,qhd->khd",
                probability.astype(jnp.bfloat16),
                ctx_grad,
                preferred_element_type=jnp.float32,
            )
            prob_grad = jnp.einsum(
                "qhd,khd->hqk", ctx_grad, value_block, preferred_element_type=jnp.float32
            )
            row_dot = jnp.sum(probability * prob_grad, axis=-1, keepdims=True)
            score_grad = (probability * (prob_grad - row_dot)).astype(jnp.bfloat16)
            block_pieces.append(
                jnp.einsum(
                    "hqk,khd->qhd", score_grad, key_block, preferred_element_type=jnp.float32
                ).astype(jnp.bfloat16)
            )
            key_totals[group_index] = key_totals[group_index] + jnp.einsum(
                "hqk,qhd->khd", score_grad, query_block, preferred_element_type=jnp.float32
            )
        query_grads.append(jnp.concatenate(block_pieces, axis=1))
    key_grads = jnp.concatenate(
        [key_total.astype(jnp.bfloat16) for key_total in key_totals], axis=1
    )
    value_grads = jnp.concatenate(
        [value_total.astype(jnp.bfloat16) for value_total in value_totals], axis=1
    )
    grad_query = jnp.concatenate(query_grads, axis=0).reshape(TOK_DEV, D) * 0.125
    grad_keys = key_grads.reshape(TOK_DEV, D)
    grad_values = value_grads.reshape(TOK_DEV, D)
    stacked_grads = jnp.stack([grad_query, grad_keys, grad_values])
    grad_qkv = jnp.einsum("td,nte->nde", tokens, stacked_grads, preferred_element_type=jnp.float32)
    input_grad = (
        grad_resid
        + jnp.einsum(
            "nte,nde->td", stacked_grads, attn_full[:3], preferred_element_type=jnp.float32
        )
    ).astype(jnp.bfloat16)
    grad_attention_full = jnp.concatenate([grad_qkv, grad_output_proj[None]], axis=0)
    vector_head = jnp.stack(
        [
            grad_gain_one,
            grad_gain_two,
            grad_shift_one,
            grad_shift_two,
            jnp.sum(grad_query.astype(jnp.float32), axis=0),
            jnp.sum(grad_values.astype(jnp.float32), axis=0),
            grad_bias_mixed,
            jnp.sum(grad_branch.astype(jnp.float32), axis=0),
        ]
    )
    grad_bias_up = jnp.sum(grad_pre_low.astype(jnp.float32), axis=0).reshape(FF // D, D)
    grad_vectors_full = jnp.concatenate([vector_head, grad_bias_up], axis=0)
    grad_attention, grad_vectors = (
        lax.psum_scatter(grad_attention_full, "fsdp", scatter_dimension=1, tiled=True),
        lax.psum_scatter(grad_vectors_full, "fsdp", scatter_dimension=1, tiled=True),
    )
    attention_new = inner_step(
        attention_weight, grad_attention, attention_first[0], attention_second[0], 0.03, 0.1
    )
    expand_new = inner_step(
        expand_weight, grad_expand, expand_first[0], expand_second[0], 0.03, 0.1
    )
    contract_new = inner_step(
        contract_weight, grad_contract, contract_first[0], contract_second[0], 0.015, 0.1
    )
    vectors_new = inner_step(vectors, grad_vectors, vectors_first[0], vectors_second[0], 0.2, 0.0)
    summed = (
        lax.psum((attention_weight - attention_new[0]).astype(jnp.bfloat16), "rep").astype(
            jnp.float32
        ),
        lax.psum((expand_weight - expand_new[0]).astype(jnp.bfloat16), "rep").astype(jnp.float32),
        lax.psum((contract_weight - contract_new[0]).astype(jnp.bfloat16), "rep").astype(
            jnp.float32
        ),
        lax.psum((vectors - vectors_new[0]).astype(jnp.bfloat16), "rep").astype(jnp.float32),
    )
    groups_count = lax.axis_size("rep")
    results = []
    for weight_now, momentum_now, inner_new, diff_total in zip(
        (attention_weight, expand_weight, contract_weight, vectors),
        (attention_momentum, expand_momentum, contract_momentum, vectors_momentum),
        (attention_new, expand_new, contract_new, vectors_new),
        summed,
    ):
        mean_diff = diff_total / groups_count
        momentum_new = 0.5 * momentum_now + mean_diff
        outer_new = weight_now - 0.7 * (mean_diff + 0.5 * momentum_new)
        results.append(
            (
                inner_new[1][None],
                inner_new[2][None],
                jnp.stack([mean_diff, momentum_new, outer_new]),
                outer_new.astype(jnp.bfloat16),
            )
        )
    return (
        layer_output.astype(jnp.bfloat16),
        input_grad,
        results[0][0],
        results[0][1],
        results[0][2],
        results[0][3],
        results[1][0],
        results[1][1],
        results[1][2],
        results[1][3],
        results[2][0],
        results[2][1],
        results[2][2],
        results[2][3],
        results[3][0],
        results[3][1],
        results[3][2],
        results[3][3],
    )


def solution(mesh):
    placed = (
        P(("rep", "fsdp"), None),
        P(("rep", "fsdp"), None),
        P(("rep", "fsdp"), None),
        P(None, "fsdp", None),
        P(None, "fsdp", None),
        P("rep", None, "fsdp", None),
        P("rep", None, "fsdp", None),
        P("fsdp", None),
        P("fsdp", None),
        P("rep", "fsdp", None),
        P("rep", "fsdp", None),
        P("fsdp", None),
        P("fsdp", None),
        P("rep", "fsdp", None),
        P("rep", "fsdp", None),
        P(None, "fsdp"),
        P(None, "fsdp"),
        P("rep", None, "fsdp"),
        P("rep", None, "fsdp"),
    )
    return jax.shard_map(
        per_device,
        mesh=mesh,
        in_specs=placed,
        out_specs=(
            P(("rep", "fsdp"), None),
            P(("rep", "fsdp"), None),
            P("rep", None, "fsdp", None),
            P("rep", None, "fsdp", None),
            P(None, None, "fsdp", None),
            P(None, "fsdp", None),
            P("rep", "fsdp", None),
            P("rep", "fsdp", None),
            P(None, "fsdp", None),
            P("fsdp", None),
            P("rep", "fsdp", None),
            P("rep", "fsdp", None),
            P(None, "fsdp", None),
            P("fsdp", None),
            P("rep", None, "fsdp"),
            P("rep", None, "fsdp"),
            P(None, None, "fsdp"),
            P(None, "fsdp"),
        ),
        check_vma=False,
    )
```

profile of v0, /device:TPU:0, one launch (start us, length us, event | category | flops | bytes accessed | tf_op | source)
XLA Modules:
  0.0 1465.5 jit_solution(9158751748262666368)
XLA Ops:
  16.3 28.9 %all_gather.13 = bf16[12,1024]{1,0:T(8,128)(2,1)S(1)} all-gather(bf16[12,128]{1,0:T(8,128)(2,1)S(1)} %convert_element_type.221), channel_id=1, replica_groups=mesh['rep'=4,'fsdp'=8] {'fsdp'}, dimensions={1}, use_global_device_ids=true | all-gather | bytes 27648 | tf_op jit(solution)/shard_map/all_gather | solution.py:88
  54.0 84.8 %all-gather.4.cloned.1.call-done = bf16[4,1024,1024]{1,2,0:T(8,128)(2,1)} async-done(((bf16[4,128,1024]{1,2,0:T(8,128)(2,1)}), bf16[4,1024,1024]{1,2,0:T(8,128)(2,1)}) %all-gather.4.cloned.1.call-update) | async-done | bytes 8388624 | tf_op jit(solution)/shard_map/all_gather | solution.py:87
  176.6 13.4 fusion.6
  217.6 13.5 fusion.8
  264.1 48.0 %multiply_convert_fusion.4 = (bf16[1024,4096]{1,0:T(8,128)(2,1)}, f32[1024,4096]{1,0:T(8,128)}, f32[1024,4096]{1,0:T(8,128)}) fusion(f32[4096]{0:T(1024)S(1)} %bitcast.308, bf16[1024,4096]{1,0:T(8,128)(2,1)} %all-gather.6.cloned.1.call-done, bf16[1024,1024]{0,1:T(8,128)(2,1)S(1)} %fusion.134.clone.4), kind=kOutput, calls=%fused_computation.17 | convolution fusion | flops 8866758656 | bytes 52445184 | tf_op jit(solution)/shard_map/dot_general | solution.py:150
  312.1 77.4 %all-gather.8.cloned.1.call-done = bf16[4096,1024]{1,0:T(8,128)(2,1)} async-done(((bf16[512,1024]{1,0:T(8,128)(2,1)}), bf16[4096,1024]{1,0:T(8,128)(2,1)}) %all-gather.8.cloned.1.call-update) | async-done | bytes 8388624 | tf_op jit(solution)/shard_map/all_gather | solution.py:148
  389.5 14.9 %fusion.141 = (f32[1024]{0:T(1024)S(1)}, f32[1024,1024]{0,1:T(8,128)S(1)}) fusion(f32[1024]{0:T(1024)S(1)} %bitcast.316, bf16[1024,4096]{1,0:T(8,128)(2,1)} %get-tuple-element.65, bf16[4096,1024]{1,0:T(8,128)(2,1)} %all-gather.8.cloned.1.call-done, f32[1024]{0:T(1024)S(1)} %bitcast.304, f32[1024]{0:T(1024)S(1)} %bitcast.294, ...), kind=kOutput, calls=%fused_computation.264 | convolution fusion | flops 8597273600 | bytes 25190400 | tf_op jit(solution)/shard_map/dot_general | solution.py:152
  414.7 24.3 %convert_reduce_fusion = (f32[4096]{0:T(1024)}, bf16[1024,4096]{1,0:T(8,128)(2,1)}) fusion(f32[1024,4096]{1,0:T(8,128)} %get-tuple-element.66, f32[1024,4096]{1,0:T(8,128)} %get-tuple-element.120, f32[4096]{0:T(1024)S(1)} %bitcast.309, bf16[1024,1024]{0,1:T(8,128)(2,1)} %get-tuple-element.60, bf16[4096,1024]{1,0:T(8,128)(2,1)} %all-gather.8.cloned.1.call-done), kind=kOutput, calls=%fused_computation.3 | convolution fusion | flops 8661233664 | bytes 52461568 | tf_op jit(solution)/shard_map/dot_general | solution.py:43
  439.0 14.9 %fusion.131 = f32[1024,4096]{1,0:T(8,128)} fusion(bf16[1024,4096]{1,0:T(8,128)(2,1)} %get-tuple-element.58, f32[1024,1024]{0,1:T(8,128)S(1)} %copy-done.7, f32[1024]{0:T(1024)S(1)} %bitcast.305, f32[1024]{0:T(1024)S(1)} %bitcast.295, f32[1024]{0:T(1024)S(1)} %add_rsqrt_fusion.1, f32[1024]{0:T(1024)S(1)} %broadcast_multiply_fusion.5), kind=kOutput, calls=%fused_computation.258 | convolution fusion | flops 8595177472 | bytes 29376512 | tf_op jit(solution)/shard_map/dot_general | solution.py:37
  455.5 19.6 %multiply_reduce_fusion.4 = (f32[1024]{0:T(1024)}, f32[1024]{0:T(1024)S(1)}, f32[1024]{0:T(1024)S(1)}, f32[1024]{0:T(1024)}, f32[1024,1024]{0,1:T(8,128)S(1)}) fusion(f32[1024,1024]{0,1:T(8,128)} %copy-done.6, f32[1024]{0:T(1024)S(1)} %add_rsqrt_fusion.1, f32[1024]{0:T(1024)S(1)} %broadcast_multiply_fusion.5, f32[1024]{0:T(1024)S(1)} %bitcast.296, ...), kind=kOutput, calls=%fused_computation.96 | convolution fusion | flops 8608804864 | bytes 31506432 | tf_op jit(solution)/shard_map/dot_general | solution.py:43
  483.0 9.9 fusion.14
  493.0 9.9 fusion.16
  509.7 10.6 fusion.81
  526.0 9.4 fusion.95
  535.5 9.3 fusion.96
  544.8 21.2 %multiply_reduce_fusion.3 = (f32[8,512]{1,0:T(8,128)}, f32[8,512]{1,0:T(8,128)}, f32[8,512,1024]{2,1,0:T(8,128)}) fusion(f32[8,512,1024]{2,1,0:T(8,128)} %get-tuple-element.116, f32[8,512]{1,0:T(8,128)} %copy-done.50, pred[512,1024]{1,0:T(8,128)(4,1)S(1)} %copy-done.11, f32[8,512,1024]{2,1,0:T(8,128)} %fusion.96, f32[8,512]{1,0:T(8,128)} %copy-done.52, ...), kind=kOutput, calls=%fused_computation.14 | convolution fusion | flops 570417152 | bytes 69271552 | tf_op jit(solution)/shard_map/qhd,khd->hqk/dot_general | solution.py:207
  566.1 24.3 %multiply_reduce_fusion.1 = (f32[8,512]{1,0:T(8,128)S(1)}, f32[8,512]{1,0:T(8,128)S(1)}, f32[8,512,1024]{2,1,0:T(8,128)}) fusion(f32[8,512,1024]{2,1,0:T(8,128)} %get-tuple-element.113, f32[8,512]{1,0:T(8,128)} %copy-done.54, pred[512,1024]{1,0:T(8,128)(4,1)S(1)} %copy-done.13, f32[8,512,1024]{2,1,0:T(8,128)} %fusion.95, f32[8,512]{1,0:T(8,128)} %copy-done.56, ...), kind=kOutput, calls=%fused_computation.8 | convolution fusion | flops 570417152 | bytes 69271552 | tf_op jit(solution)/shard_map/qhd,khd->hqk/dot_general | solution.py:207
  590.5 52.7 %multiply_convert_fusion.1 = (bf16[8,512,1024]{2,1,0:T(8,128)(2,1)}, bf16[8,512,1024]{2,1,0:T(8,128)(2,1)S(1)}, bf16[8,512,1024]{2,1,0:T(8,128)(2,1)}, bf16[8,512,1024]{2,1,0:T(8,128)(2,1)}) fusion(f32[8,512,1024]{2,1,0:T(8,128)} %get-tuple-element.125, f32[8,512,1024]{2,1,0:T(8,128)} %get-tuple-element.113, f32[8,512]{1,0:T(8,128)S(1)} %get-tuple-element.44, ...), kind=kLoop, calls=%fused_computation.7 | loop fusion | flops 83886080 | bytes 168951808 | tf_op jit(solution)/shard_map/convert_element_type | solution.py:211
  710.0 14.9 %fusion.142 = f32[4096,1024]{1,0:T(8,128)} fusion(bf16[1024,4096]{1,0:T(8,128)(2,1)} %get-tuple-element.65, bf16[1024,1024]{0,1:T(8,128)(2,1)S(1)} %copy-done.45), kind=kOutput, calls=%fused_computation.265 | convolution fusion | flops 8589934592 | bytes 27262976 | tf_op jit(solution)/shard_map/dot_general | solution.py:37
  748.9 266.6 %reduce-scatter.5.cloned.1.call-done = f32[4,128,1024]{1,2,0:T(8,128)} async-done(((f32[4,1024,1024]{1,2,0:T(8,128)}), f32[4,128,1024]{1,2,0:T(8,128)}) %reduce-scatter.5.cloned.1.call-update) | async-done | bytes 2097168 | tf_op jit(solution)/shard_map/reduce_scatter | solution.py:254
  1021.7 276.8 %reduce-scatter.9.cloned.1.call-done = f32[512,1024]{1,0:T(8,128)} async-done(((f32[4096,1024]{1,0:T(8,128)}), f32[512,1024]{1,0:T(8,128)}) %reduce-scatter.9.cloned.1.call-update) | async-done | bytes 2097168 | tf_op jit(solution)/shard_map/reduce_scatter | solution.py:166
  1306.4 13.0 fusion.47
  1323.4 32.2 %reduce-scatter.11.cloned.1.call-done = f32[12,128]{1,0:T(8,128)} async-done(((f32[12,1024]{1,0:T(8,128)}), f32[12,128]{1,0:T(8,128)}) %reduce-scatter.11.cloned.1.call-update) | async-done | bytes 6160 | tf_op jit(solution)/shard_map/reduce_scatter | solution.py:255
  1370.4 56.4 %all-reduce.3.cloned.1.call-done = (bf16[4,128,1024]{1,2,0:T(8,128)(2,1)}, bf16[128,4096]{1,0:T(8,128)(2,1)}, bf16[512,1024]{1,0:T(8,128)(2,1)}) async-done(((bf16[4,128,1024]{1,2,0:T(8,128)(2,1)}, bf16[128,4096]{1,0:T(8,128)(2,1)}, bf16[512,1024]{1,0:T(8,128)(2,1)}), (bf16[4,128,1024]{1,2,0:T(8,128)(2,1)}, bf16[128,4096]{1,0:T(8,128)(2,1)}, bf16[512,1024]{1,0:T(8,128)(2,1)})) %all-reduce.3.cloned.1.call-update) | async-done | bytes 3145744 | tf_op jit(solution)/shard_map/psum | solution.py:268
  (337 shorter events, 302.3 us)
Async XLA Ops:
  7.2 131.6 %all-gather.4.cloned.1.call-start = ((), (), s32[]{:S(2)}) async-start(), calls=%async_computation.4 | async-start | bytes 9437184 | tf_op jit(solution)/shard_map/all_gather | solution.py:87
  10.5 35.4 %copy-start.84 = (s32[1,1024]{1,0:T(1,128)S(1)}, s32[1,1024]{1,0:T(1,128)}, u32[]{:S(2)}) copy-start(s32[1,1024]{1,0:T(1,128)} %param.21) | copy-start | bytes 12292
  10.5 253.7 %all-gather.6.cloned.1.call-start = ((), (), s32[]{:S(2)}) async-start(), calls=%async_computation.5 | async-start | bytes 9437184 | tf_op jit(solution)/shard_map/all_gather | solution.py:147
  13.3 376.3 %all-gather.8.cloned.1.call-start = ((), (), s32[]{:S(2)}) async-start(), calls=%async_computation.6 | async-start | bytes 9437184 | tf_op jit(solution)/shard_map/all_gather | solution.py:148
  13.3 33.4 %copy-start.36 = (bf16[1024,1024]{1,0:T(8,128)(2,1)S(1)}, bf16[1024,1024]{1,0:T(8,128)(2,1)}, u32[]{:S(2)}) copy-start(bf16[1024,1024]{1,0:T(8,128)(2,1)} %param.20) | copy-start | bytes 6291460
  16.2 724.2 %reduce-scatter.7.cloned.1.call-start = ((), (), s32[]{:S(2)}) async-start(), calls=%async_computation.8 | async-start | bytes 18874368 | tf_op jit(solution)/shard_map/reduce_scatter | solution.py:165
  49.2 89.5 %copy-start.37 = (bf16[1024,1024]{1,0:T(8,128)(2,1)S(1)}, bf16[1024,1024]{1,0:T(8,128)(2,1)}, u32[]{:S(2)}) copy-start(bf16[1024,1024]{1,0:T(8,128)(2,1)} %param.19) | copy-start | bytes 6291460
  54.0 154.6 %copy-start.10 = (pred[512,1024]{1,0:T(8,128)(4,1)}, pred[512,1024]{1,0:T(8,128)(4,1)S(1)}, u32[]{:S(2)}) copy-start(pred[512,1024]{1,0:T(8,128)(4,1)S(1)} %get-tuple-element.108) | copy-start | bytes 1572868
  54.0 193.1 %copy-start.12 = (pred[512,1024]{1,0:T(8,128)(4,1)}, pred[512,1024]{1,0:T(8,128)(4,1)S(1)}, u32[]{:S(2)}) copy-start(pred[512,1024]{1,0:T(8,128)(4,1)S(1)} %get-tuple-element.109) | copy-start | bytes 1572868
  152.7 64.9 %copy-start.4 = (bf16[1,1024,1024]{1,2,0:T(8,128)(2,1)}, bf16[1,1024,1024]{1,2,0:T(8,128)(2,1)S(1)}, u32[]{:S(2)}) copy-start(bf16[1,1024,1024]{1,2,0:T(8,128)(2,1)S(1)} %slice.220) | copy-start | bytes 6291460
  158.2 59.4 %copy-start.16 = (bf16[1,1024,16,64]{1,3,2,0:T(8,128)(2,1)}, bf16[1,1024,16,64]{1,3,2,0:T(8,128)(2,1)S(1)}, u32[]{:S(2)}) copy-start(bf16[1,1024,16,64]{1,3,2,0:T(8,128)(2,1)S(1)} %multiply_convert_fusion.5) | copy-start | bytes 6291460
  166.6 80.5 %copy-start.58 = (f32[8,512]{1,0:T(8,128)}, f32[8,512]{1,0:T(8,128)S(1)}, u32[]{:S(2)}) copy-start(f32[8,512]{1,0:T(8,128)S(1)} %get-tuple-element.112) | copy-start | bytes 49156
  175.0 33.6 %copy-start.60 = (f32[8,512]{1,0:T(8,128)}, f32[8,512]{1,0:T(8,128)S(1)}, u32[]{:S(2)}) copy-start(f32[8,512]{1,0:T(8,128)S(1)} %get-tuple-element.115) | copy-start | bytes 49156
  264.1 125.4 %copy-start.94 = (f32[1,1024]{1,0:T(1,128)S(1)}, f32[1,1024]{1,0:T(1,128)}, u32[]{:S(2)}) copy-start(f32[1,1024]{1,0:T(1,128)} %get-tuple-element.99) | copy-start | bytes 12292
  454.0 561.5 %reduce-scatter.5.cloned.1.call-start = ((), (), s32[]{:S(2)}) async-start(), calls=%async_computation.7 | async-start | bytes 18874368 | tf_op jit(solution)/shard_map/reduce_scatter | solution.py:254
  475.2 34.4 %copy-start.50 = (f32[8,512]{1,0:T(8,128)}, f32[8,512]{1,0:T(8,128)S(1)}, u32[]{:S(2)}) copy-start(f32[8,512]{1,0:T(8,128)S(1)} %log_add_fusion.3) | copy-start | bytes 49156
  708.5 590.0 %reduce-scatter.9.cloned.1.call-start = ((), (), s32[]{:S(2)}) async-start(), calls=%async_computation.9 | async-start | bytes 18874368 | tf_op jit(solution)/shard_map/reduce_scatter | solution.py:166
  724.9 630.6 %reduce-scatter.11.cloned.1.call-start = ((), (), s32[]{:S(2)}) async-start(), calls=%async_computation.10 | async-start | bytes 73728 | tf_op jit(solution)/shard_map/reduce_scatter | solution.py:255
  740.1 275.4 %copy-start.15 = (f32[4,128,1024]{1,2,0:T(8,128)S(1)}, f32[4,128,1024]{1,2,0:T(8,128)}, u32[]{:S(2)}) copy-start(f32[4,128,1024]{1,2,0:T(8,128)} %copy-done.14) | copy-start | bytes 6291460
  740.1 686.7 %all-reduce.3.cloned.1.call-start = ((), (), s32[]{:S(2)}) async-start(), calls=%async_computation.11 | async-start | bytes 6291456 | tf_op jit(solution)/shard_map/psum | solution.py:268
  1319.4 36.2 %copy-start.67 = (f32[12,128]{1,0:T(8,128)S(1)}, f32[12,128]{1,0:T(8,128)}, u32[]{:S(2)}) copy-start(f32[12,128]{1,0:T(8,128)} %param.34) | copy-start | bytes 18436
  1319.4 36.2 %copy-start.90 = (f32[1,12,128]{2,0,1:T(1,128)S(1)}, f32[1,12,128]{2,0,1:T(1,128)}, u32[]{:S(2)}) copy-start(f32[1,12,128]{2,0,1:T(1,128)} %param.36) | copy-start | bytes 18436
  1319.4 36.2 %copy-start.91 = (f32[1,12,128]{2,0,1:T(1,128)S(1)}, f32[1,12,128]{2,0,1:T(1,128)}, u32[]{:S(2)}) copy-start(f32[1,12,128]{2,0,1:T(1,128)} %param.37) | copy-start | bytes 18436
  1319.4 44.0 %copy-start.89 = (f32[12,128]{1,0:T(8,128)S(1)}, f32[12,128]{1,0:T(8,128)}, u32[]{:S(2)}) copy-start(f32[12,128]{1,0:T(8,128)} %param.35) | copy-start | bytes 18436
  (92 other events, 930.0 us)
Sparse Core Ops, SparseCore 0:
  10.6 128.0 all-gather.3
  141.4 122.6 all-gather.5
  266.8 122.6 all-gather.7
  454.1 278.3 reduce-scatter.6
  736.1 279.3 reduce-scatter.4
  1019.1 279.3 reduce-scatter.8
  1301.6 53.9 reduce-scatter.10
  1359.3 67.5 all-reduce.2
where the time goes:
time: 1480 us; the launch traced here: 1470 us
  waiting for transfers between devices  796 us (54%)
  matrix products  386 us (26%)
  other arithmetic  150 us (10%)
  local copies, waits for them, and re-layouts  82.1 us (6%)
  blocking collectives  34.9 us (2%)
  between operations  16 us (1%)
    reduce_scatter x1, waiting for transfers between devices, per_device(): lax.psum_scatter(contract_full, 'fsdp', scatter_dimension=0, tiled=True)  277 us
    reduce_scatter x1, waiting for transfers between devices, per_device(): lax.psum_scatter(grad_attention_full, 'fsdp', scatter_dimension=1, tiled=...  267 us
    all_gather x1, waiting for transfers between devices, per_device(): lax.all_gather(attention_weight.astype(jnp.bfloat16), 'fsdp', axis=1, til...  84.8 us
    all_gather x1, waiting for transfers between devices, per_device(): lax.all_gather(contract_weight.astype(jnp.bfloat16), 'fsdp', axis=0, tile...  77.4 us
    dot_general x4, matrix products, per_device(): jnp.einsum('qhd,khd->hqk', ctx_grad, value_block, preferred_element_type=...  64.3 us
    unnamed x230, local copies, waits for them, and re-layouts  62 us
    psum x1, waiting for transfers between devices, per_device(): lax.psum((attention_weight - attention_new[0]).astype(jnp.bfloat16), 'rep')  56.4 us
    convert_element_type x1, other arithmetic, per_device(): score_grad = (probability * (prob_grad - row_dot)).astype(jnp.bfloat16)  52.7 us
  transfers between devices with their start and end apart: 8, of which 7 were waited for; matrix products, arithmetic and copies ran while one was open for 34% of the time, Pallas kernels for 0%

commit v1 on v0

--- a/solution.py
+++ b/solution.py
@@ -12,6 +12,7 @@
 SEQ_DEV = 1
 ADAM_STEP = 4
 TOK_DEV = 1024
+_step_on_stages_all = lambda s0, mesh_dim: jnp.sum(jax.lax.all_gather(s0, mesh_dim), axis=0)
 
 
 def norm_forward(values_in, gain_row, shift_row):
@@ -265,9 +266,9 @@
     )
     vectors_new = inner_step(vectors, grad_vectors, vectors_first[0], vectors_second[0], 0.2, 0.0)
     summed = (
-        lax.psum((attention_weight - attention_new[0]).astype(jnp.bfloat16), "rep").astype(
-            jnp.float32
-        ),
+        _step_on_stages_all(
+            (attention_weight - attention_new[0]).astype(jnp.bfloat16), "rep"
+        ).astype(jnp.float32),
         lax.psum((expand_weight - expand_new[0]).astype(jnp.bfloat16), "rep").astype(jnp.float32),
         lax.psum((contract_weight - contract_new[0]).astype(jnp.bfloat16), "rep").astype(
             jnp.float32

time: 1480 us -> 1480 us (level)
    all_gather x0 -> x1, waiting for transfers between devices: none -> 22.4 us  [jax.lax.all_gather(s0, mesh_dim)]
    psum x1, waiting for transfers between devices: 56.4 us -> 38.6 us  [per_device(): lax.psum((expand_weight - expand_new[0]).astype(jnp.bfloat16), 'rep')]
    unnamed x230 -> x212, local copies, waits for them, and re-layouts: 62 us -> 59.1 us
  transfers between devices with their start and end apart: 8 -> 9, of which waited for: 7 -> 8; matrix products, arithmetic and copies ran while one was open for 34% -> 35% of each run, Pallas kernels for 0% -> 0%
where the time goes in v1:
time: 1480 us; the launch traced here: 1470 us
  waiting for transfers between devices  796 us (54%)
  matrix products  386 us (26%)
  other arithmetic  154 us (10%)
  local copies, waits for them, and re-layouts  83.5 us (6%)
  blocking collectives  34.9 us (2%)
  between operations  15.6 us (1%)
    reduce_scatter x1, waiting for transfers between devices, per_device(): lax.psum_scatter(contract_full, 'fsdp', scatter_dimension=0, tiled=True)  276 us
    reduce_scatter x1, waiting for transfers between devices, per_device(): lax.psum_scatter(grad_attention_full, 'fsdp', scatter_dimension=1, tiled=...  270 us
    all_gather x1, waiting for transfers between devices, per_device(): lax.all_gather(attention_weight.astype(jnp.bfloat16), 'fsdp', axis=1, til...  84.9 us
    all_gather x1, waiting for transfers between devices, per_device(): lax.all_gather(contract_weight.astype(jnp.bfloat16), 'fsdp', axis=0, tile...  77.1 us
    dot_general x4, matrix products, per_device(): jnp.einsum('qhd,khd->hqk', ctx_grad, value_block, preferred_element_type=...  63.8 us
    unnamed x212, local copies, waits for them, and re-layouts  59.1 us
    convert_element_type x1, other arithmetic, per_device(): score_grad = (probability * (prob_grad - row_dot)).astype(jnp.bfloat16)  52.5 us
    dot_general x3, matrix products, product_back(): lax.dot_general(left, right, (((1,), (1,)), ((), ())), preferred_element_...  49.1 us
  transfers between devices with their start and end apart: 9, of which 8 were waited for; matrix products, arithmetic and copies ran while one was open for 35% of the time, Pallas kernels for 0%

profile of v1, /device:TPU:0, one launch (start us, length us, event | category | flops | bytes accessed | tf_op | source)
XLA Modules:
  0.0 1471.2 jit_solution(12136680983258783926)
XLA Ops:
  16.3 28.9 %all_gather.19 = bf16[12,1024]{1,0:T(8,128)(2,1)S(1)} all-gather(bf16[12,128]{1,0:T(8,128)(2,1)S(1)} %convert_element_type.231), channel_id=1, replica_groups=mesh['rep'=4,'fsdp'=8] {'fsdp'}, dimensions={1}, use_global_device_ids=true | all-gather | bytes 27648 | tf_op jit(solution)/shard_map/all_gather | solution.py:89
  53.8 84.9 %all-gather.6.cloned.1.call-done = bf16[4,1024,1024]{1,2,0:T(8,128)(2,1)} async-done(((bf16[4,128,1024]{1,2,0:T(8,128)(2,1)}), bf16[4,1024,1024]{1,2,0:T(8,128)(2,1)}) %all-gather.6.cloned.1.call-update) | async-done | bytes 8388624 | tf_op jit(solution)/shard_map/all_gather | solution.py:88
  138.7 9.7 convolution_bitcast_fusion.1
  167.6 13.5 fusion.6
  219.0 13.8 fusion.8
  264.6 47.8 %multiply_convert_fusion.4 = (bf16[1024,4096]{1,0:T(8,128)(2,1)}, f32[1024,4096]{1,0:T(8,128)}, f32[1024,4096]{1,0:T(8,128)}) fusion(f32[4096]{0:T(1024)S(1)} %bitcast.312, bf16[1024,4096]{1,0:T(8,128)(2,1)} %all-gather.8.cloned.1.call-done, bf16[1024,1024]{0,1:T(8,128)(2,1)S(1)} %fusion.134.clone.4), kind=kOutput, calls=%fused_computation.17 | convolution fusion | flops 8866758656 | bytes 52445184 | tf_op jit(solution)/shard_map/dot_general | solution.py:151
  312.4 77.1 %all-gather.10.cloned.1.call-done = bf16[4096,1024]{1,0:T(8,128)(2,1)} async-done(((bf16[512,1024]{1,0:T(8,128)(2,1)}), bf16[4096,1024]{1,0:T(8,128)(2,1)}) %all-gather.10.cloned.1.call-update) | async-done | bytes 8388624 | tf_op jit(solution)/shard_map/all_gather | solution.py:149
  389.5 15.1 %fusion.141 = (f32[1024]{0:T(1024)S(1)}, f32[1024,1024]{0,1:T(8,128)S(1)}) fusion(f32[1024]{0:T(1024)S(1)} %bitcast.320, bf16[1024,4096]{1,0:T(8,128)(2,1)} %get-tuple-element.100, bf16[4096,1024]{1,0:T(8,128)(2,1)} %all-gather.10.cloned.1.call-done, f32[1024]{0:T(1024)S(1)} %bitcast.307, f32[1024]{0:T(1024)S(1)} %bitcast.298, ...), kind=kOutput, calls=%fused_computation.264 | convolution fusion | flops 8597273600 | bytes 25190400 | tf_op jit(solution)/shard_map/dot_general | solution.py:153
  414.6 24.6 %convert_reduce_fusion = (f32[4096]{0:T(1024)}, bf16[1024,4096]{1,0:T(8,128)(2,1)}) fusion(f32[1024,4096]{1,0:T(8,128)} %get-tuple-element.101, f32[1024,4096]{1,0:T(8,128)} %get-tuple-element.155, f32[4096]{0:T(1024)S(1)} %bitcast.313, bf16[1024,1024]{0,1:T(8,128)(2,1)} %get-tuple-element.95, bf16[4096,1024]{1,0:T(8,128)(2,1)} %all-gather.10.cloned.1.call-done), kind=kOutput, calls=%fused_computation.3 | convolution fusion | flops 8661233664 | bytes 52461568 | tf_op jit(solution)/shard_map/dot_general | solution.py:44
  439.3 15.0 %fusion.131 = f32[1024,4096]{1,0:T(8,128)} fusion(bf16[1024,4096]{1,0:T(8,128)(2,1)} %get-tuple-element.93, f32[1024,1024]{0,1:T(8,128)S(1)} %copy-done.6, f32[1024]{0:T(1024)S(1)} %bitcast.308, f32[1024]{0:T(1024)S(1)} %bitcast.299, f32[1024]{0:T(1024)S(1)} %add_rsqrt_fusion.1, f32[1024]{0:T(1024)S(1)} %broadcast_multiply_fusion.5), kind=kOutput, calls=%fused_computation.258 | convolution fusion | flops 8595177472 | bytes 29376512 | tf_op jit(solution)/shard_map/dot_general | solution.py:38
  455.8 15.2 %fusion.142 = f32[4096,1024]{1,0:T(8,128)} fusion(bf16[1024,4096]{1,0:T(8,128)(2,1)} %get-tuple-element.100, bf16[1024,1024]{0,1:T(8,128)(2,1)S(1)} %copy-done.39), kind=kOutput, calls=%fused_computation.265 | convolution fusion | flops 8589934592 | bytes 27262976 | tf_op jit(solution)/shard_map/dot_general | solution.py:38
  472.6 18.8 %multiply_reduce_fusion.4 = (f32[1024]{0:T(1024)}, f32[1024]{0:T(1024)S(1)}, f32[1024]{0:T(1024)S(1)}, f32[1024]{0:T(1024)}, f32[1024,1024]{0,1:T(8,128)S(1)}) fusion(f32[1024,1024]{0,1:T(8,128)} %copy-done.5, f32[1024]{0:T(1024)S(1)} %add_rsqrt_fusion.1, f32[1024]{0:T(1024)S(1)} %broadcast_multiply_fusion.5, f32[1024]{0:T(1024)S(1)} %bitcast.300, ...), kind=kOutput, calls=%fused_computation.96 | convolution fusion | flops 8608804864 | bytes 31506432 | tf_op jit(solution)/shard_map/dot_general | solution.py:44
  519.2 21.0 %multiply_reduce_fusion.3 = (f32[8,512]{1,0:T(8,128)}, f32[8,512]{1,0:T(8,128)}, f32[8,512,1024]{2,1,0:T(8,128)}) fusion(f32[8,512,1024]{2,1,0:T(8,128)} %get-tuple-element.151, f32[8,512]{1,0:T(8,128)} %log_add_fusion.3, pred[512,1024]{1,0:T(8,128)(4,1)S(1)} %copy-done.10, f32[8,512,1024]{2,1,0:T(8,128)} %fusion.96, f32[8,512]{1,0:T(8,128)} %log_add_fusion.2, ...), kind=kOutput, calls=%fused_computation.14 | convolution fusion | flops 570417152 | bytes 69271552 | tf_op jit(solution)/shard_map/qhd,khd->hqk/dot_general | solution.py:208
  540.2 25.4 %multiply_reduce_fusion.1 = (f32[8,512]{1,0:T(8,128)S(1)}, f32[8,512]{1,0:T(8,128)S(1)}, f32[8,512,1024]{2,1,0:T(8,128)}) fusion(f32[8,512,1024]{2,1,0:T(8,128)} %get-tuple-element.148, f32[8,512]{1,0:T(8,128)} %log_add_fusion.1, pred[512,1024]{1,0:T(8,128)(4,1)S(1)} %copy-done.12, f32[8,512,1024]{2,1,0:T(8,128)} %fusion.95, f32[8,512]{1,0:T(8,128)} %log_add_fusion, ...), kind=kOutput, calls=%fused_computation.8 | convolution fusion | flops 570417152 | bytes 69271552 | tf_op jit(solution)/shard_map/qhd,khd->hqk/dot_general | solution.py:208
  565.6 52.5 %multiply_convert_fusion.1 = (bf16[8,512,1024]{2,1,0:T(8,128)(2,1)}, bf16[8,512,1024]{2,1,0:T(8,128)(2,1)S(1)}, bf16[8,512,1024]{2,1,0:T(8,128)(2,1)}, bf16[8,512,1024]{2,1,0:T(8,128)(2,1)}) fusion(f32[8,512,1024]{2,1,0:T(8,128)} %get-tuple-element.160, f32[8,512,1024]{2,1,0:T(8,128)} %get-tuple-element.148, f32[8,512]{1,0:T(8,128)S(1)} %get-tuple-element.80, ...), kind=kLoop, calls=%fused_computation.7 | loop fusion | flops 83886080 | bytes 168951808 | tf_op jit(solution)/shard_map/convert_element_type | solution.py:212
  618.2 9.7 fusion.87
  674.6 9.5 fusion.14
  684.1 10.6 fusion.81
  739.8 276.0 %reduce-scatter.9.cloned.1.call-done = f32[512,1024]{1,0:T(8,128)} async-done(((f32[4096,1024]{1,0:T(8,128)}), f32[512,1024]{1,0:T(8,128)}) %reduce-scatter.9.cloned.1.call-update) | async-done | bytes 2097168 | tf_op jit(solution)/shard_map/reduce_scatter | solution.py:167
  1029.2 269.6 %reduce-scatter.5.cloned.1.call-done = f32[4,128,1024]{1,2,0:T(8,128)} async-done(((f32[4,1024,1024]{1,2,0:T(8,128)}), f32[4,128,1024]{1,2,0:T(8,128)}) %reduce-scatter.5.cloned.1.call-update) | async-done | bytes 2097168 | tf_op jit(solution)/shard_map/reduce_scatter | solution.py:255
  1309.5 12.9 fusion.47
  1330.3 25.5 %reduce-scatter.11.cloned.1.call-done = f32[12,128]{1,0:T(8,128)} async-done(((f32[12,1024]{1,0:T(8,128)}), f32[12,128]{1,0:T(8,128)}) %reduce-scatter.11.cloned.1.call-update) | async-done | bytes 6160 | tf_op jit(solution)/shard_map/reduce_scatter | solution.py:256
  1370.7 38.6 %all-reduce.3.cloned.1.call-done = (bf16[128,4096]{1,0:T(8,128)(2,1)}, bf16[512,1024]{1,0:T(8,128)(2,1)}) async-done(((bf16[128,4096]{1,0:T(8,128)(2,1)}, bf16[512,1024]{1,0:T(8,128)(2,1)}), (bf16[128,4096]{1,0:T(8,128)(2,1)}, bf16[512,1024]{1,0:T(8,128)(2,1)})) %all-reduce.3.cloned.1.call-update) | async-done | bytes 2097168 | tf_op jit(solution)/shard_map/psum | solution.py:272
  1423.6 22.4 %all-gather.12.cloned.1.call-done = bf16[16,128,1024]{2,1,0:T(8,128)(2,1)} async-done(((bf16[4,128,1024]{2,1,0:T(8,128)(2,1)}), bf16[16,128,1024]{2,1,0:T(8,128)(2,1)}) %all-gather.12.cloned.1.call-update) | async-done | bytes 4194320 | tf_op jit(solution)/shard_map/all_gather | solution.py:15
  (326 shorter events, 317.5 us)
Async XLA Ops:
  7.2 131.5 %all-gather.6.cloned.1.call-start = ((), (), s32[]{:S(2)}) async-start(), calls=%async_computation.4 | async-start | bytes 9437184 | tf_op jit(solution)/shard_map/all_gather | solution.py:88
  10.4 35.5 %copy-start.73 = (s32[1,1024]{1,0:T(1,128)S(1)}, s32[1,1024]{1,0:T(1,128)}, u32[]{:S(2)}) copy-start(s32[1,1024]{1,0:T(1,128)} %param.21) | copy-start | bytes 12292
  10.4 254.1 %all-gather.8.cloned.1.call-start = ((), (), s32[]{:S(2)}) async-start(), calls=%async_computation.5 | async-start | bytes 9437184 | tf_op jit(solution)/shard_map/all_gather | solution.py:148
  13.2 376.3 %all-gather.10.cloned.1.call-start = ((), (), s32[]{:S(2)}) async-start(), calls=%async_computation.6 | async-start | bytes 9437184 | tf_op jit(solution)/shard_map/all_gather | solution.py:149
  13.3 37.3 %copy-start.32 = (bf16[1024,1024]{1,0:T(8,128)(2,1)S(1)}, bf16[1024,1024]{1,0:T(8,128)(2,1)}, u32[]{:S(2)}) copy-start(bf16[1024,1024]{1,0:T(8,128)(2,1)} %param.20) | copy-start | bytes 6291460
  16.2 716.7 %reduce-scatter.7.cloned.1.call-start = ((), (), s32[]{:S(2)}) async-start(), calls=%async_computation.8 | async-start | bytes 18874368 | tf_op jit(solution)/shard_map/reduce_scatter | solution.py:166
  53.8 147.7 %copy-start.9 = (pred[512,1024]{1,0:T(8,128)(4,1)}, pred[512,1024]{1,0:T(8,128)(4,1)S(1)}, u32[]{:S(2)}) copy-start(pred[512,1024]{1,0:T(8,128)(4,1)S(1)} %get-tuple-element.143) | copy-start | bytes 1572868
  53.8 195.0 %copy-start.11 = (pred[512,1024]{1,0:T(8,128)(4,1)}, pred[512,1024]{1,0:T(8,128)(4,1)S(1)}, u32[]{:S(2)}) copy-start(pred[512,1024]{1,0:T(8,128)(4,1)S(1)} %get-tuple-element.144) | copy-start | bytes 1572868
  158.8 60.2 %copy-start.3 = (bf16[1,1024,1024]{1,2,0:T(8,128)(2,1)}, bf16[1,1024,1024]{1,2,0:T(8,128)(2,1)S(1)}, u32[]{:S(2)}) copy-start(bf16[1,1024,1024]{1,2,0:T(8,128)(2,1)S(1)} %slice.220) | copy-start | bytes 6291460
  159.2 59.7 %copy-start.15 = (bf16[1,1024,16,64]{1,3,2,0:T(8,128)(2,1)}, bf16[1,1024,16,64]{1,3,2,0:T(8,128)(2,1)S(1)}, u32[]{:S(2)}) copy-start(bf16[1,1024,16,64]{1,3,2,0:T(8,128)(2,1)S(1)} %multiply_convert_fusion.5) | copy-start | bytes 6291460
  167.6 33.9 %copy-start.47 = (f32[8,512]{1,0:T(8,128)}, f32[8,512]{1,0:T(8,128)S(1)}, u32[]{:S(2)}) copy-start(f32[8,512]{1,0:T(8,128)S(1)} %get-tuple-element.150) | copy-start | bytes 49156
  218.9 29.9 %copy-start.53 = (f32[8,512]{1,0:T(8,128)}, f32[8,512]{1,0:T(8,128)S(1)}, u32[]{:S(2)}) copy-start(f32[8,512]{1,0:T(8,128)S(1)} %get-tuple-element.147) | copy-start | bytes 49156
  264.6 125.0 %copy-start.83 = (f32[1,1024]{1,0:T(1,128)S(1)}, f32[1,1024]{1,0:T(1,128)}, u32[]{:S(2)}) copy-start(f32[1,1024]{1,0:T(1,128)} %get-tuple-element.134) | copy-start | bytes 12292
  454.3 561.6 %reduce-scatter.9.cloned.1.call-start = ((), (), s32[]{:S(2)}) async-start(), calls=%async_computation.9 | async-start | bytes 18874368 | tf_op jit(solution)/shard_map/reduce_scatter | solution.py:167
  471.1 827.6 %reduce-scatter.5.cloned.1.call-start = ((), (), s32[]{:S(2)}) async-start(), calls=%async_computation.7 | async-start | bytes 18874368 | tf_op jit(solution)/shard_map/reduce_scatter | solution.py:255
  727.6 628.2 %reduce-scatter.11.cloned.1.call-start = ((), (), s32[]{:S(2)}) async-start(), calls=%async_computation.10 | async-start | bytes 73728 | tf_op jit(solution)/shard_map/reduce_scatter | solution.py:256
  730.6 285.2 %copy-start.21 = (f32[512,1024]{1,0:T(8,128)S(1)}, f32[512,1024]{1,0:T(8,128)}, u32[]{:S(2)}) copy-start(f32[512,1024]{1,0:T(8,128)} %param.30) | copy-start | bytes 6291460
  730.7 678.6 %all-reduce.3.cloned.1.call-start = ((), (), s32[]{:S(2)}) async-start(), calls=%async_computation.12 | async-start | bytes 4194304 | tf_op jit(solution)/shard_map/psum | solution.py:272
  1023.1 275.6 %copy-start.14 = (f32[4,128,1024]{1,2,0:T(8,128)S(1)}, f32[4,128,1024]{1,2,0:T(8,128)}, u32[]{:S(2)}) copy-start(f32[4,128,1024]{1,2,0:T(8,128)} %copy-done.13) | copy-start | bytes 6291460
  1023.1 422.9 %all-gather.12.cloned.1.call-start = ((), (), s32[]{:S(2)}) async-start(), calls=%async_computation.11 | async-start | bytes 5242880 | tf_op jit(solution)/shard_map/all_gather | solution.py:15
  1322.4 33.5 %copy-start.56 = (f32[12,128]{1,0:T(8,128)S(1)}, f32[12,128]{1,0:T(8,128)}, u32[]{:S(2)}) copy-start(f32[12,128]{1,0:T(8,128)} %param.34) | copy-start | bytes 18436
  1322.4 33.5 %copy-start.79 = (f32[1,12,128]{2,0,1:T(1,128)S(1)}, f32[1,12,128]{2,0,1:T(1,128)}, u32[]{:S(2)}) copy-start(f32[1,12,128]{2,0,1:T(1,128)} %param.36) | copy-start | bytes 18436
  1322.4 33.5 %copy-start.80 = (f32[1,12,128]{2,0,1:T(1,128)S(1)}, f32[1,12,128]{2,0,1:T(1,128)}, u32[]{:S(2)}) copy-start(f32[1,12,128]{2,0,1:T(1,128)} %param.37) | copy-start | bytes 18436
  1322.4 41.3 %copy-start.78 = (f32[12,128]{1,0:T(8,128)S(1)}, f32[12,128]{1,0:T(8,128)}, u32[]{:S(2)}) copy-start(f32[12,128]{1,0:T(8,128)} %param.35) | copy-start | bytes 18436
  (84 other events, 870.8 us)
Sparse Core Ops, SparseCore 0:
  10.6 128.0 all-gather.5
  141.4 122.6 all-gather.7
  266.8 122.6 all-gather.9
  454.4 278.3 reduce-scatter.6
  736.5 279.3 reduce-scatter.8
  1019.5 279.2 reduce-scatter.4
  1301.9 53.9 reduce-scatter.10
  1358.8 50.4 all-reduce.2
  1411.4 34.5 all-gather.11
